TPU v7x, 32 devices: a whole 2x2x4 slice. The times are simulated.
32 devices in a mesh: groups: 2 (over y), section: 4 (over z), seq: 4 (over x, core).
Axes of the slice: x: 2, y: 2, z: 4, core: 2. Of those that a mesh axis runs over, the one named last changes fastest.
Arguments:
- tokens: bfloat16 [8, 256, 1440], P('groups', 'seq'), parts along dimension 0, may hold values from -6 to 6
- block_order: int32 [8], P('groups'), parts along dimension 0, may hold values from 0 to 3, each once
- prompt_lengths: int32 [8], P('groups'), parts along dimension 0, may hold values from 1 to 256, 576 in all
- norm_gain: float32 [4, 1440], P('section'), may hold values from 0.1 to 1.9
- w_query: bfloat16 [4, 1440, 2048], P('section', None, 'seq'), may hold values from -4 to 4
- w_key_value: bfloat16 [4, 1440, 512], P('section'), may hold values from -4 to 4
- w_out: bfloat16 [4, 2048, 1440], P('section', 'seq'), may hold values from -0.125 to 0.125
- sink_logits: float32 [4, 32], P('section'), may hold values from 0 to 4
Outputs:
- hidden_states: bfloat16 [4, 8, 256, 1440], P('section', 'groups', 'seq'), parts along dimension 1
- layer_cache: bfloat16 [4, 8, 256, 512], P('section', 'groups', 'seq'), parts along dimension 1
There are 2 independent parts, one for each index of `groups`. A program takes and returns all parts, laid end to end along the dimension named above; an argument that names none is the same for every part. Nothing has to cross between parts.
Inputs may be any that keep to these rules, and one draw needn't show every extreme that they name: `block_order`: each of 0 to 3 exactly once. `prompt_lengths`: the longest prompt is full.
All inputs are finite; a program needn't handle non-finite values.
Results may differ from a plain program's by a relative error of at most 0.024.
Values may be sent and summed in bfloat16 or wider, within the bound.
No kernel may reach another device: no remote copies, remote signals or barrier semaphores. Data moves between devices by JAX's collectives and lax.ppermute only.
A program may use at most 128 MiB of HBM per device.

v0:
```python
import math
import jax
import jax.numpy as jnp
from jax import lax
from jax.sharding import PartitionSpec as P

HEAD_DIM = 64
WIN = 128
THETA = 150000.0
EPSILON = 1e-05


def from_behind(block, axis, distance):
    devices = range(lax.axis_size(axis))
    route = [(i - distance, i) for i in devices if i - distance in devices]
    return lax.ppermute(block, axis, route)


def rotary(positions, head_size):
    half = head_size // 2
    freq = jnp.exp(jnp.arange(half, dtype=jnp.float32) * (-2.0 * math.log(THETA) / head_size))
    angles = positions.astype(jnp.float32)[:, None] * freq[None, :]
    return (jnp.cos(angles)[:, None, :], jnp.sin(angles)[:, None, :])


def rotate(values, cosine, sine):
    half = values.shape[-1] // 2
    first = values[..., :half]
    second = values[..., half:]
    return jnp.concatenate([first * cosine - second * sine, second * cosine + first * sine], -1)


def per_device(
    tokens, block_order, prompt_lengths, norm_gain, w_query, w_key_value, w_out, sink_logits
):
    section_index = lax.axis_index("section")
    sections = lax.axis_size("section")
    seq_index = lax.axis_index("seq")
    micro, rows, width = tokens.shape
    full_query, full_out = (
        lax.all_gather(w_query, "seq", axis=2, tiled=True),
        lax.all_gather(w_out, "seq", axis=1, tiled=True),
    )
    query_weight = full_query[0]
    out_weight = full_out[0]
    pair_weight = w_key_value[0]
    gain = norm_gain[0]
    heads_width = query_weight.shape[1]
    head_count = heads_width // HEAD_DIM
    kv_width = pair_weight.shape[1] // 2
    kv_heads = kv_width // HEAD_DIM
    group = head_count // kv_heads
    sink = sink_logits[0].reshape(kv_heads, group)[:, :, None]
    keep = min(WIN, rows)
    depth = WIN // keep
    start = seq_index * rows
    positions = start + jnp.arange(rows, dtype=jnp.int32)
    cosine, sine = rotary(positions, HEAD_DIM)
    key_positions = start - WIN + jnp.arange(WIN + rows, dtype=jnp.int32)

    def project(hidden):
        widened = hidden.astype(jnp.float32)
        scale = lax.rsqrt(jnp.mean(widened * widened, -1, keepdims=True) + EPSILON)
        normed = (widened * scale * gain).astype(jnp.bfloat16)
        queries = jnp.dot(normed, query_weight, preferred_element_type=jnp.float32).reshape(
            rows, head_count, HEAD_DIM
        )
        queries = rotate(queries, cosine, sine).astype(jnp.bfloat16).reshape(rows, heads_width)
        projected = jnp.dot(normed, pair_weight, preferred_element_type=jnp.float32)
        rotated = rotate(
            projected[:, :kv_width].reshape(rows, kv_heads, HEAD_DIM), cosine, sine
        ).reshape(rows, kv_width)
        cache = jnp.concatenate([rotated, projected[:, kv_width:]], 1).astype(jnp.bfloat16)
        return (queries, cache)

    def project_spare(hidden):
        return (
            jnp.zeros((rows, heads_width), jnp.bfloat16),
            jnp.zeros((rows, 2 * kv_width), jnp.bfloat16),
        )

    def window_of(cache):
        pieces = [from_behind(cache, "seq", offset) for offset in range(depth, 0, -1)]
        return jnp.concatenate(pieces, 0)

    def attend(operands):
        hidden, queries, cache, window, length = operands
        joined = jnp.concatenate([window, cache], 0)
        key_heads = joined[:, :kv_width].reshape(WIN + rows, kv_heads, HEAD_DIM)
        value_heads = joined[:, kv_width:].reshape(WIN + rows, kv_heads, HEAD_DIM)
        grouped = queries.reshape(rows, kv_heads, group, HEAD_DIM)
        scores = (
            jnp.einsum("qkgd,skd->kgqs", grouped, key_heads, preferred_element_type=jnp.float32)
            * 0.125
        )
        query_col = positions[:, None]
        key_row = key_positions[None, :]
        allowed = (key_row <= query_col) & (query_col - key_row < WIN) & (key_row >= 0)
        allowed = allowed & ((key_row < length) | (key_row == query_col))
        masked = jnp.where(allowed, scores, jnp.float32(-1e30))
        top = jnp.maximum(jnp.max(masked, -1), sink)
        expo = jnp.where(allowed, jnp.exp(scores - top[..., None]), jnp.float32(0.0))
        total = jnp.sum(expo, -1) + jnp.exp(sink - top)
        weights = (expo / total[..., None]).astype(jnp.bfloat16)
        context = jnp.einsum(
            "kgqs,skd->qkgd", weights, value_heads, preferred_element_type=jnp.float32
        )
        context = context.reshape(rows, heads_width).astype(jnp.bfloat16)
        output = jnp.dot(context, out_weight, preferred_element_type=jnp.float32)
        return (hidden.astype(jnp.float32) + output).astype(jnp.bfloat16)

    def pass_through(operands):
        return operands[0]

    def turn(counter, carry):
        arriving, hidden_buffer, cache_buffer = carry
        slot = counter - section_index
        active = (slot >= 0) & (slot < micro)
        slot_safe = jnp.clip(slot, 0, micro - 1)
        block = block_order[slot_safe]
        length = prompt_lengths[block]
        entering = lax.dynamic_index_in_dim(tokens, block, 0, keepdims=False)
        hidden = jnp.where(section_index == 0, entering, arriving)
        queries, cache = lax.cond(active, project, project_spare, hidden)
        window = window_of(cache)
        updated = lax.cond(active, attend, pass_through, (hidden, queries, cache, window, length))
        previous_hidden = lax.dynamic_index_in_dim(hidden_buffer, slot_safe, 0, keepdims=False)
        previous_cache = lax.dynamic_index_in_dim(cache_buffer, slot_safe, 0, keepdims=False)
        hidden_buffer = lax.dynamic_update_index_in_dim(
            hidden_buffer, jnp.where(active, updated, previous_hidden), slot_safe, 0
        )
        cache_buffer = lax.dynamic_update_index_in_dim(
            cache_buffer, jnp.where(active, cache, previous_cache), slot_safe, 0
        )
        passed = from_behind(updated, "section", 1)
        return (passed, hidden_buffer, cache_buffer)

    initial = (
        jnp.zeros((rows, width), jnp.bfloat16),
        jnp.zeros((micro, rows, width), jnp.bfloat16),
        jnp.zeros((micro, rows, 2 * kv_width), jnp.bfloat16),
    )
    final = lax.fori_loop(0, micro + sections - 1, turn, initial)
    return (final[1][None], final[2][None])


def solution(mesh):
    in_specs = (
        P("groups", "seq", None),
        P("groups"),
        P("groups"),
        P("section", None),
        P("section", None, "seq"),
        P("section", None, None),
        P("section", "seq", None),
        P("section", None),
    )
    out_specs = (P("section", "groups", "seq", None), P("section", "groups", "seq", None))
    return jax.shard_map(
        per_device, mesh=mesh, in_specs=in_specs, out_specs=out_specs, check_vma=False
    )
```

profile of v0, /device:TPU:28, one launch (start us, length us, event | category | flops | bytes accessed | tf_op | source)
XLA Modules:
  0.0 363.9 jit_solution(2830805438816558788)
XLA Ops:
  8.5 1.6 copy.14
  11.5 43.2 %all-gather.3.cloned.1.call-done = bf16[1,1440,2048]{2,1,0:T(8,128)(2,1)} async-done(((bf16[1,1440,512]{2,1,0:T(8,128)(2,1)}), bf16[1,1440,2048]{2,1,0:T(8,128)(2,1)}) %all-gather.3.cloned.1.call-update) | async-done | bytes 5898256 | tf_op jit(solution)/shard_map/all_gather | solution.py:41
  54.6 47.9 %all-gather.5.cloned.1.call-done = bf16[1,2048,1440]{2,1,0:T(8,128)(2,1)} async-done(((bf16[1,512,1440]{2,1,0:T(8,128)(2,1)}), bf16[1,2048,1440]{2,1,0:T(8,128)(2,1)}) %all-gather.5.cloned.1.call-update) | async-done | bytes 5898256 | tf_op jit(solution)/shard_map/all_gather | solution.py:42
  104.3 252.8 %while.20 = (s32[]{:T(128)}, bf16[64,1440]{1,0:T(8,128)(2,1)S(1)}, bf16[4,64,1440]{2,1,0:T(8,128)(2,1)}, bf16[4,64,512]{2,1,0:T(8,128)(2,1)}, s32[]{:T(128)}, /*...) while((s32[]{:T(128)}, bf16[64,1440]{1,0:T(8,128)(2,1)S(1)}, ...), condition=%wide.region_8.9_spmd.clone.clone, body=%wide.region_0.8_spmd.clone.clone.sunk | while | flops 958372544 | bytes 47880768 | solution.py:143
  107.8 1.4 conditional.8
  109.1 2.5 collective-permute-start
  111.6 1.9 collective-permute-start.1
  116.0 1.3 collective-permute-start.2
  118.0 7.3 %collective-permute-done.2 = bf16[64,1440]{1,0:T(8,128)(2,1)S(1)} collective-permute-done((bf16[64,1440]{1,0:T(8,128)(2,1)S(1)}, bf16[64,1440]{1,0:T(8,128)(2,1)S(1)}, u32[]{:S(2)}, u32[]{:S(2)}) %collective-permute-start.2) | collective-permute-done | bytes 184352 | tf_op jit(solution)/shard_map/while/body/eval_jaxpr/ppermute | solution.py:16
  128.8 1.4 conditional.8
  130.1 3.0 collective-permute-start
  133.2 1.3 collective-permute-start.1
  137.0 1.3 collective-permute-start.2
  139.0 7.2 %collective-permute-done.2 = bf16[64,1440]{1,0:T(8,128)(2,1)S(1)} collective-permute-done((bf16[64,1440]{1,0:T(8,128)(2,1)S(1)}, bf16[64,1440]{1,0:T(8,128)(2,1)S(1)}, u32[]{:S(2)}, u32[]{:S(2)}) %collective-permute-start.2) | collective-permute-done | bytes 184352 | tf_op jit(solution)/shard_map/while/body/eval_jaxpr/ppermute | solution.py:16
  149.6 1.4 conditional.8
  151.0 3.0 collective-permute-start
  154.0 1.3 collective-permute-start.1
  157.8 1.3 collective-permute-start.2
  159.8 50.5 %collective-permute-done.2 = bf16[64,1440]{1,0:T(8,128)(2,1)S(1)} collective-permute-done((bf16[64,1440]{1,0:T(8,128)(2,1)S(1)}, bf16[64,1440]{1,0:T(8,128)(2,1)S(1)}, u32[]{:S(2)}, u32[]{:S(2)}) %collective-permute-start.2) | collective-permute-done | bytes 184352 | tf_op jit(solution)/shard_map/while/body/eval_jaxpr/ppermute | solution.py:16
  213.8 9.2 %conditional.8 = (bf16[64,2048]{1,0:T(8,128)(2,1)S(1)}, bf16[64,512]{1,0:T(8,128)(2,1)}, bf16[64,512]{0,1:T(8,128)(2,1)}) conditional(s32[]{:T(128)} %convert_element_type.69, () %tuple.79, (bf16[64,1440]{1,0:T(8,128)(2,1)S(1)}, f32[1,1440]{1,0:T(1,128)S(1)}, bf16[1440,2048]{1,0:T(8,128)(2,1)}, f32[64,1,32]{2,0,1:T(8,128)S(1)}, ...), branch_computations={%region_1.1_spmd, %region_2.3_spmd} | conditional | flops 474183744 | bytes 12373788 | solution.py:124
  214.0 3.9 %fusion.26 = f32[64,2048]{1,0:T(8,128)S(1)} fusion(bf16[1440,2048]{1,0:T(8,128)(2,1)} %get-tuple-element.374, bf16[64,1440]{1,0:T(8,128)(2,1)S(1)} %get-tuple-element.372, f32[1440]{0:T(1024)S(1)} %reduce, f32[64]{0:T(128)S(1)} %add_rsqrt_fusion), kind=kOutput, calls=%fused_computation.44 | convolution fusion | flops 377856000 | bytes 6612864 | tf_op jit(solution)/shard_map/while/body/eval_jaxpr/cond/branch_1_fun/dot_general | solution.py:65
  221.4 1.6 copy.18
  223.0 2.3 collective-permute-start
  225.4 1.3 collective-permute-start.1
  228.5 1.5 bitcast_dynamic-update-slice_fusion.5
  230.0 8.0 %conditional.9 = (bf16[64,1440]{1,0:T(8,128)(2,1)S(1)}) conditional(s32[]{:T(128)} %convert_element_type.69, bf16[64,1440]{1,0:T(8,128)(2,1)S(1)} %bitcast_select_fusion.5, (bf16[64,1440]{1,0:T(8,128)(2,1)S(1)}, bf16[64,512]{0,1:T(8,128)(2,1)S(1)}, bf16[64,512]{0,1:T(8,128)(2,1)S(1)}, bf16[64,512]{1,0:T(8,128)(2,1)}, s32[]{:T(128)}, ...), branch_computations={%region_4.4_spmd, %region_5.7_spmd} | conditional | flops 483969664 | bytes 32420688 | solution.py:126
  234.5 1.1 convolution_convert_fusion
  236.7 1.2 fusion.8
  238.0 1.3 collective-permute-start.2
  240.0 7.1 %collective-permute-done.2 = bf16[64,1440]{1,0:T(8,128)(2,1)S(1)} collective-permute-done((bf16[64,1440]{1,0:T(8,128)(2,1)S(1)}, bf16[64,1440]{1,0:T(8,128)(2,1)S(1)}, u32[]{:S(2)}, u32[]{:S(2)}) %collective-permute-start.2) | collective-permute-done | bytes 184352 | tf_op jit(solution)/shard_map/while/body/eval_jaxpr/ppermute | solution.py:16
  250.6 9.2 %conditional.8 = (bf16[64,2048]{1,0:T(8,128)(2,1)S(1)}, bf16[64,512]{1,0:T(8,128)(2,1)}, bf16[64,512]{0,1:T(8,128)(2,1)}) conditional(s32[]{:T(128)} %convert_element_type.69, () %tuple.79, (bf16[64,1440]{1,0:T(8,128)(2,1)S(1)}, f32[1,1440]{1,0:T(1,128)S(1)}, bf16[1440,2048]{1,0:T(8,128)(2,1)}, f32[64,1,32]{2,0,1:T(8,128)S(1)}, ...), branch_computations={%region_1.1_spmd, %region_2.3_spmd} | conditional | flops 474183744 | bytes 12373788 | solution.py:124
  250.8 3.9 %fusion.26 = f32[64,2048]{1,0:T(8,128)S(1)} fusion(bf16[1440,2048]{1,0:T(8,128)(2,1)} %get-tuple-element.374, bf16[64,1440]{1,0:T(8,128)(2,1)S(1)} %get-tuple-element.372, f32[1440]{0:T(1024)S(1)} %reduce, f32[64]{0:T(128)S(1)} %add_rsqrt_fusion), kind=kOutput, calls=%fused_computation.44 | convolution fusion | flops 377856000 | bytes 6612864 | tf_op jit(solution)/shard_map/while/body/eval_jaxpr/cond/branch_1_fun/dot_general | solution.py:65
  258.2 1.6 copy.18
  259.8 2.3 collective-permute-start
  262.1 1.3 collective-permute-start.1
  265.2 1.5 bitcast_dynamic-update-slice_fusion.5
  266.7 8.0 %conditional.9 = (bf16[64,1440]{1,0:T(8,128)(2,1)S(1)}) conditional(s32[]{:T(128)} %convert_element_type.69, bf16[64,1440]{1,0:T(8,128)(2,1)S(1)} %bitcast_select_fusion.5, (bf16[64,1440]{1,0:T(8,128)(2,1)S(1)}, bf16[64,512]{0,1:T(8,128)(2,1)S(1)}, bf16[64,512]{0,1:T(8,128)(2,1)S(1)}, bf16[64,512]{1,0:T(8,128)(2,1)}, s32[]{:T(128)}, ...), branch_computations={%region_4.4_spmd, %region_5.7_spmd} | conditional | flops 483969664 | bytes 32420688 | solution.py:126
  266.7 1.0 copy.13
  271.3 1.1 convolution_convert_fusion
  273.5 1.2 fusion.8
  274.7 1.3 collective-permute-start.2
  276.8 7.1 %collective-permute-done.2 = bf16[64,1440]{1,0:T(8,128)(2,1)S(1)} collective-permute-done((bf16[64,1440]{1,0:T(8,128)(2,1)S(1)}, bf16[64,1440]{1,0:T(8,128)(2,1)S(1)}, u32[]{:S(2)}, u32[]{:S(2)}) %collective-permute-start.2) | collective-permute-done | bytes 184352 | tf_op jit(solution)/shard_map/while/body/eval_jaxpr/ppermute | solution.py:16
  287.3 9.2 %conditional.8 = (bf16[64,2048]{1,0:T(8,128)(2,1)S(1)}, bf16[64,512]{1,0:T(8,128)(2,1)}, bf16[64,512]{0,1:T(8,128)(2,1)}) conditional(s32[]{:T(128)} %convert_element_type.69, () %tuple.79, (bf16[64,1440]{1,0:T(8,128)(2,1)S(1)}, f32[1,1440]{1,0:T(1,128)S(1)}, bf16[1440,2048]{1,0:T(8,128)(2,1)}, f32[64,1,32]{2,0,1:T(8,128)S(1)}, ...), branch_computations={%region_1.1_spmd, %region_2.3_spmd} | conditional | flops 474183744 | bytes 12373788 | solution.py:124
  287.5 3.9 %fusion.26 = f32[64,2048]{1,0:T(8,128)S(1)} fusion(bf16[1440,2048]{1,0:T(8,128)(2,1)} %get-tuple-element.374, bf16[64,1440]{1,0:T(8,128)(2,1)S(1)} %get-tuple-element.372, f32[1440]{0:T(1024)S(1)} %reduce, f32[64]{0:T(128)S(1)} %add_rsqrt_fusion), kind=kOutput, calls=%fused_computation.44 | convolution fusion | flops 377856000 | bytes 6612864 | tf_op jit(solution)/shard_map/while/body/eval_jaxpr/cond/branch_1_fun/dot_general | solution.py:65
  294.9 1.6 copy.18
  296.5 2.3 collective-permute-start
  298.9 1.3 collective-permute-start.1
  302.0 1.5 bitcast_dynamic-update-slice_fusion.5
  303.5 8.0 %conditional.9 = (bf16[64,1440]{1,0:T(8,128)(2,1)S(1)}) conditional(s32[]{:T(128)} %convert_element_type.69, bf16[64,1440]{1,0:T(8,128)(2,1)S(1)} %bitcast_select_fusion.5, (bf16[64,1440]{1,0:T(8,128)(2,1)S(1)}, bf16[64,512]{0,1:T(8,128)(2,1)S(1)}, bf16[64,512]{0,1:T(8,128)(2,1)S(1)}, bf16[64,512]{1,0:T(8,128)(2,1)}, s32[]{:T(128)}, ...), branch_computations={%region_4.4_spmd, %region_5.7_spmd} | conditional | flops 483969664 | bytes 32420688 | solution.py:126
  308.0 1.1 convolution_convert_fusion
  310.2 1.2 fusion.8
  311.5 1.3 collective-permute-start.2
  313.5 7.1 %collective-permute-done.2 = bf16[64,1440]{1,0:T(8,128)(2,1)S(1)} collective-permute-done((bf16[64,1440]{1,0:T(8,128)(2,1)S(1)}, bf16[64,1440]{1,0:T(8,128)(2,1)S(1)}, u32[]{:S(2)}, u32[]{:S(2)}) %collective-permute-start.2) | collective-permute-done | bytes 184352 | tf_op jit(solution)/shard_map/while/body/eval_jaxpr/ppermute | solution.py:16
  324.1 9.2 %conditional.8 = (bf16[64,2048]{1,0:T(8,128)(2,1)S(1)}, bf16[64,512]{1,0:T(8,128)(2,1)}, bf16[64,512]{0,1:T(8,128)(2,1)}) conditional(s32[]{:T(128)} %convert_element_type.69, () %tuple.79, (bf16[64,1440]{1,0:T(8,128)(2,1)S(1)}, f32[1,1440]{1,0:T(1,128)S(1)}, bf16[1440,2048]{1,0:T(8,128)(2,1)}, f32[64,1,32]{2,0,1:T(8,128)S(1)}, ...), branch_computations={%region_1.1_spmd, %region_2.3_spmd} | conditional | flops 474183744 | bytes 12373788 | solution.py:124
  324.3 3.9 %fusion.26 = f32[64,2048]{1,0:T(8,128)S(1)} fusion(bf16[1440,2048]{1,0:T(8,128)(2,1)} %get-tuple-element.374, bf16[64,1440]{1,0:T(8,128)(2,1)S(1)} %get-tuple-element.372, f32[1440]{0:T(1024)S(1)} %reduce, f32[64]{0:T(128)S(1)} %add_rsqrt_fusion), kind=kOutput, calls=%fused_computation.44 | convolution fusion | flops 377856000 | bytes 6612864 | tf_op jit(solution)/shard_map/while/body/eval_jaxpr/cond/branch_1_fun/dot_general | solution.py:65
  331.7 1.6 copy.18
  333.3 2.3 collective-permute-start
  335.6 1.3 collective-permute-start.1
  338.7 1.5 bitcast_dynamic-update-slice_fusion.5
  340.2 8.0 %conditional.9 = (bf16[64,1440]{1,0:T(8,128)(2,1)S(1)}) conditional(s32[]{:T(128)} %convert_element_type.69, bf16[64,1440]{1,0:T(8,128)(2,1)S(1)} %bitcast_select_fusion.5, (bf16[64,1440]{1,0:T(8,128)(2,1)S(1)}, bf16[64,512]{0,1:T(8,128)(2,1)S(1)}, bf16[64,512]{0,1:T(8,128)(2,1)S(1)}, bf16[64,512]{1,0:T(8,128)(2,1)}, s32[]{:T(128)}, ...), branch_computations={%region_4.4_spmd, %region_5.7_spmd} | conditional | flops 483969664 | bytes 32420688 | solution.py:126
  344.8 1.1 convolution_convert_fusion
  347.0 1.2 fusion.8
  348.2 1.3 collective-permute-start.2
  350.3 6.8 %collective-permute-done.2 = bf16[64,1440]{1,0:T(8,128)(2,1)S(1)} collective-permute-done((bf16[64,1440]{1,0:T(8,128)(2,1)S(1)}, bf16[64,1440]{1,0:T(8,128)(2,1)S(1)}, u32[]{:S(2)}, u32[]{:S(2)}) %collective-permute-start.2) | collective-permute-done | bytes 184352 | tf_op jit(solution)/shard_map/while/body/eval_jaxpr/ppermute | solution.py:16
  (244 shorter events, 75.3 us)
Async XLA Ops:
  7.2 1.4 copy-start.1
  7.2 47.5 %all-gather.3.cloned.1.call-start = ((), (), s32[]{:S(2)}) async-start(), calls=%async_computation | async-start | bytes 7372800 | tf_op jit(solution)/shard_map/all_gather | solution.py:41
  7.9 2.8 copy-start.3
  7.9 94.7 %all-gather.5.cloned.1.call-start = ((), (), s32[]{:S(2)}) async-start(), calls=%async_computation.1 | async-start | bytes 7864320 | tf_op jit(solution)/shard_map/all_gather | solution.py:42
  10.2 94.1 %copy-start = (bf16[1,1440,512]{2,1,0:T(8,128)(2,1)S(1)}, bf16[1,1440,512]{2,1,0:T(8,128)(2,1)}, u32[]{:S(2)}) copy-start(bf16[1,1440,512]{2,1,0:T(8,128)(2,1)} %param.19) | copy-start | bytes 4423684
  10.2 94.1 %copy-start.2 = (f32[1,1440]{1,0:T(1,128)S(1)}, f32[1,1440]{1,0:T(1,128)}, u32[]{:S(2)}) copy-start(f32[1,1440]{1,0:T(1,128)} %param.17) | copy-start | bytes 17284
  10.2 94.1 %copy-start.4 = (s32[4]{0:T(128)S(1)}, s32[4]{0:T(128)}, u32[]{:S(2)}) copy-start(s32[4]{0:T(128)} %param.15) | copy-start | bytes 52
  10.2 94.1 %copy-start.5 = (s32[4]{0:T(128)S(1)}, s32[4]{0:T(128)}, u32[]{:S(2)}) copy-start(s32[4]{0:T(128)} %param.16) | copy-start | bytes 52
  109.1 6.8 %collective-permute-start = (bf16[64,512]{0,1:T(8,128)(2,1)}, bf16[64,512]{0,1:T(8,128)(2,1)S(1)}, u32[]{:S(2)}, u32[]{:S(2)}) collective-permute-start(bf16[64,512]{0,1:T(8,128)(2,1)} %get-tuple-element.696), channel_id=1, source_target_pairs={{0,2},{1,3},{4,6},{5,7},{8,10},{9,11},{12,14},{13,15},{16,18},{17,... | collective-permute-start | bytes 196616 | tf_op jit(solution)/shard_map/while/body/eval_jaxpr/ppermute | solution.py:16
  111.6 4.3 %collective-permute-start.1 = (bf16[64,512]{0,1:T(8,128)(2,1)}, bf16[64,512]{0,1:T(8,128)(2,1)S(1)}, u32[]{:S(2)}, u32[]{:S(2)}) collective-permute-start(bf16[64,512]{0,1:T(8,128)(2,1)} %get-tuple-element.696), channel_id=1, source_target_pairs={{0,1},{1,2},{2,3},{4,5},{5,6},{6,7},{8,9},{9,10},{10,11},{12,13},{... | collective-permute-start | bytes 196616 | tf_op jit(solution)/shard_map/while/body/eval_jaxpr/ppermute | solution.py:16
  116.0 9.3 %collective-permute-start.2 = (bf16[64,1440]{1,0:T(8,128)(2,1)S(1)}, bf16[64,1440]{1,0:T(8,128)(2,1)S(1)}, u32[]{:S(2)}, u32[]{:S(2)}) collective-permute-start(bf16[64,1440]{1,0:T(8,128)(2,1)S(1)} %get-tuple-element.771), channel_id=1, source_target_pairs={{0,4},{4,8},{8,12},{1,5},{5,9},{9,13},{2,6},{6,10},{10,14},{3,7},{... | collective-permute-start | bytes 552968 | tf_op jit(solution)/shard_map/while/body/eval_jaxpr/ppermute | solution.py:16
  130.1 6.8 %collective-permute-start = (bf16[64,512]{0,1:T(8,128)(2,1)}, bf16[64,512]{0,1:T(8,128)(2,1)S(1)}, u32[]{:S(2)}, u32[]{:S(2)}) collective-permute-start(bf16[64,512]{0,1:T(8,128)(2,1)} %get-tuple-element.696), channel_id=1, source_target_pairs={{0,2},{1,3},{4,6},{5,7},{8,10},{9,11},{12,14},{13,15},{16,18},{17,... | collective-permute-start | bytes 196616 | tf_op jit(solution)/shard_map/while/body/eval_jaxpr/ppermute | solution.py:16
  133.2 3.8 %collective-permute-start.1 = (bf16[64,512]{0,1:T(8,128)(2,1)}, bf16[64,512]{0,1:T(8,128)(2,1)S(1)}, u32[]{:S(2)}, u32[]{:S(2)}) collective-permute-start(bf16[64,512]{0,1:T(8,128)(2,1)} %get-tuple-element.696), channel_id=1, source_target_pairs={{0,1},{1,2},{2,3},{4,5},{5,6},{6,7},{8,9},{9,10},{10,11},{12,13},{... | collective-permute-start | bytes 196616 | tf_op jit(solution)/shard_map/while/body/eval_jaxpr/ppermute | solution.py:16
  137.0 9.2 %collective-permute-start.2 = (bf16[64,1440]{1,0:T(8,128)(2,1)S(1)}, bf16[64,1440]{1,0:T(8,128)(2,1)S(1)}, u32[]{:S(2)}, u32[]{:S(2)}) collective-permute-start(bf16[64,1440]{1,0:T(8,128)(2,1)S(1)} %get-tuple-element.771), channel_id=1, source_target_pairs={{0,4},{4,8},{8,12},{1,5},{5,9},{9,13},{2,6},{6,10},{10,14},{3,7},{... | collective-permute-start | bytes 552968 | tf_op jit(solution)/shard_map/while/body/eval_jaxpr/ppermute | solution.py:16
  151.0 6.8 %collective-permute-start = (bf16[64,512]{0,1:T(8,128)(2,1)}, bf16[64,512]{0,1:T(8,128)(2,1)S(1)}, u32[]{:S(2)}, u32[]{:S(2)}) collective-permute-start(bf16[64,512]{0,1:T(8,128)(2,1)} %get-tuple-element.696), channel_id=1, source_target_pairs={{0,2},{1,3},{4,6},{5,7},{8,10},{9,11},{12,14},{13,15},{16,18},{17,... | collective-permute-start | bytes 196616 | tf_op jit(solution)/shard_map/while/body/eval_jaxpr/ppermute | solution.py:16
  154.0 3.8 %collective-permute-start.1 = (bf16[64,512]{0,1:T(8,128)(2,1)}, bf16[64,512]{0,1:T(8,128)(2,1)S(1)}, u32[]{:S(2)}, u32[]{:S(2)}) collective-permute-start(bf16[64,512]{0,1:T(8,128)(2,1)} %get-tuple-element.696), channel_id=1, source_target_pairs={{0,1},{1,2},{2,3},{4,5},{5,6},{6,7},{8,9},{9,10},{10,11},{12,13},{... | collective-permute-start | bytes 196616 | tf_op jit(solution)/shard_map/while/body/eval_jaxpr/ppermute | solution.py:16
  157.8 52.5 %collective-permute-start.2 = (bf16[64,1440]{1,0:T(8,128)(2,1)S(1)}, bf16[64,1440]{1,0:T(8,128)(2,1)S(1)}, u32[]{:S(2)}, u32[]{:S(2)}) collective-permute-start(bf16[64,1440]{1,0:T(8,128)(2,1)S(1)} %get-tuple-element.771), channel_id=1, source_target_pairs={{0,4},{4,8},{8,12},{1,5},{5,9},{9,13},{2,6},{6,10},{10,14},{3,7},{... | collective-permute-start | bytes 552968 | tf_op jit(solution)/shard_map/while/body/eval_jaxpr/ppermute | solution.py:16
  223.0 6.9 %collective-permute-start = (bf16[64,512]{0,1:T(8,128)(2,1)}, bf16[64,512]{0,1:T(8,128)(2,1)S(1)}, u32[]{:S(2)}, u32[]{:S(2)}) collective-permute-start(bf16[64,512]{0,1:T(8,128)(2,1)} %get-tuple-element.696), channel_id=1, source_target_pairs={{0,2},{1,3},{4,6},{5,7},{8,10},{9,11},{12,14},{13,15},{16,18},{17,... | collective-permute-start | bytes 196616 | tf_op jit(solution)/shard_map/while/body/eval_jaxpr/ppermute | solution.py:16
  225.4 4.6 %collective-permute-start.1 = (bf16[64,512]{0,1:T(8,128)(2,1)}, bf16[64,512]{0,1:T(8,128)(2,1)S(1)}, u32[]{:S(2)}, u32[]{:S(2)}) collective-permute-start(bf16[64,512]{0,1:T(8,128)(2,1)} %get-tuple-element.696), channel_id=1, source_target_pairs={{0,1},{1,2},{2,3},{4,5},{5,6},{6,7},{8,9},{9,10},{10,11},{12,13},{... | collective-permute-start | bytes 196616 | tf_op jit(solution)/shard_map/while/body/eval_jaxpr/ppermute | solution.py:16
  233.7 2.2 slice-start
  234.5 2.2 slice-start.1
  238.0 9.1 %collective-permute-start.2 = (bf16[64,1440]{1,0:T(8,128)(2,1)S(1)}, bf16[64,1440]{1,0:T(8,128)(2,1)S(1)}, u32[]{:S(2)}, u32[]{:S(2)}) collective-permute-start(bf16[64,1440]{1,0:T(8,128)(2,1)S(1)} %get-tuple-element.771), channel_id=1, source_target_pairs={{0,4},{4,8},{8,12},{1,5},{5,9},{9,13},{2,6},{6,10},{10,14},{3,7},{... | collective-permute-start | bytes 552968 | tf_op jit(solution)/shard_map/while/body/eval_jaxpr/ppermute | solution.py:16
  259.8 6.9 %collective-permute-start = (bf16[64,512]{0,1:T(8,128)(2,1)}, bf16[64,512]{0,1:T(8,128)(2,1)S(1)}, u32[]{:S(2)}, u32[]{:S(2)}) collective-permute-start(bf16[64,512]{0,1:T(8,128)(2,1)} %get-tuple-element.696), channel_id=1, source_target_pairs={{0,2},{1,3},{4,6},{5,7},{8,10},{9,11},{12,14},{13,15},{16,18},{17,... | collective-permute-start | bytes 196616 | tf_op jit(solution)/shard_map/while/body/eval_jaxpr/ppermute | solution.py:16
  262.1 4.6 %collective-permute-start.1 = (bf16[64,512]{0,1:T(8,128)(2,1)}, bf16[64,512]{0,1:T(8,128)(2,1)S(1)}, u32[]{:S(2)}, u32[]{:S(2)}) collective-permute-start(bf16[64,512]{0,1:T(8,128)(2,1)} %get-tuple-element.696), channel_id=1, source_target_pairs={{0,1},{1,2},{2,3},{4,5},{5,6},{6,7},{8,9},{9,10},{10,11},{12,13},{... | collective-permute-start | bytes 196616 | tf_op jit(solution)/shard_map/while/body/eval_jaxpr/ppermute | solution.py:16
  270.4 2.2 slice-start
  271.3 2.2 slice-start.1
  274.7 9.1 %collective-permute-start.2 = (bf16[64,1440]{1,0:T(8,128)(2,1)S(1)}, bf16[64,1440]{1,0:T(8,128)(2,1)S(1)}, u32[]{:S(2)}, u32[]{:S(2)}) collective-permute-start(bf16[64,1440]{1,0:T(8,128)(2,1)S(1)} %get-tuple-element.771), channel_id=1, source_target_pairs={{0,4},{4,8},{8,12},{1,5},{5,9},{9,13},{2,6},{6,10},{10,14},{3,7},{... | collective-permute-start | bytes 552968 | tf_op jit(solution)/shard_map/while/body/eval_jaxpr/ppermute | solution.py:16
  296.5 6.9 %collective-permute-start = (bf16[64,512]{0,1:T(8,128)(2,1)}, bf16[64,512]{0,1:T(8,128)(2,1)S(1)}, u32[]{:S(2)}, u32[]{:S(2)}) collective-permute-start(bf16[64,512]{0,1:T(8,128)(2,1)} %get-tuple-element.696), channel_id=1, source_target_pairs={{0,2},{1,3},{4,6},{5,7},{8,10},{9,11},{12,14},{13,15},{16,18},{17,... | collective-permute-start | bytes 196616 | tf_op jit(solution)/shard_map/while/body/eval_jaxpr/ppermute | solution.py:16
  298.9 4.6 %collective-permute-start.1 = (bf16[64,512]{0,1:T(8,128)(2,1)}, bf16[64,512]{0,1:T(8,128)(2,1)S(1)}, u32[]{:S(2)}, u32[]{:S(2)}) collective-permute-start(bf16[64,512]{0,1:T(8,128)(2,1)} %get-tuple-element.696), channel_id=1, source_target_pairs={{0,1},{1,2},{2,3},{4,5},{5,6},{6,7},{8,9},{9,10},{10,11},{12,13},{... | collective-permute-start | bytes 196616 | tf_op jit(solution)/shard_map/while/body/eval_jaxpr/ppermute | solution.py:16
  307.1 2.2 slice-start
  308.0 2.2 slice-start.1
  311.5 9.1 %collective-permute-start.2 = (bf16[64,1440]{1,0:T(8,128)(2,1)S(1)}, bf16[64,1440]{1,0:T(8,128)(2,1)S(1)}, u32[]{:S(2)}, u32[]{:S(2)}) collective-permute-start(bf16[64,1440]{1,0:T(8,128)(2,1)S(1)} %get-tuple-element.771), channel_id=1, source_target_pairs={{0,4},{4,8},{8,12},{1,5},{5,9},{9,13},{2,6},{6,10},{10,14},{3,7},{... | collective-permute-start | bytes 552968 | tf_op jit(solution)/shard_map/while/body/eval_jaxpr/ppermute | solution.py:16
  333.3 6.9 %collective-permute-start = (bf16[64,512]{0,1:T(8,128)(2,1)}, bf16[64,512]{0,1:T(8,128)(2,1)S(1)}, u32[]{:S(2)}, u32[]{:S(2)}) collective-permute-start(bf16[64,512]{0,1:T(8,128)(2,1)} %get-tuple-element.696), channel_id=1, source_target_pairs={{0,2},{1,3},{4,6},{5,7},{8,10},{9,11},{12,14},{13,15},{16,18},{17,... | collective-permute-start | bytes 196616 | tf_op jit(solution)/shard_map/while/body/eval_jaxpr/ppermute | solution.py:16
  335.6 4.6 %collective-permute-start.1 = (bf16[64,512]{0,1:T(8,128)(2,1)}, bf16[64,512]{0,1:T(8,128)(2,1)S(1)}, u32[]{:S(2)}, u32[]{:S(2)}) collective-permute-start(bf16[64,512]{0,1:T(8,128)(2,1)} %get-tuple-element.696), channel_id=1, source_target_pairs={{0,1},{1,2},{2,3},{4,5},{5,6},{6,7},{8,9},{9,10},{10,11},{12,13},{... | collective-permute-start | bytes 196616 | tf_op jit(solution)/shard_map/while/body/eval_jaxpr/ppermute | solution.py:16
  343.9 2.2 slice-start
  344.8 2.2 slice-start.1
  348.2 8.8 %collective-permute-start.2 = (bf16[64,1440]{1,0:T(8,128)(2,1)S(1)}, bf16[64,1440]{1,0:T(8,128)(2,1)S(1)}, u32[]{:S(2)}, u32[]{:S(2)}) collective-permute-start(bf16[64,1440]{1,0:T(8,128)(2,1)S(1)} %get-tuple-element.771), channel_id=1, source_target_pairs={{0,4},{4,8},{8,12},{1,5},{5,9},{9,13},{2,6},{6,10},{10,14},{3,7},{... | collective-permute-start | bytes 552968 | tf_op jit(solution)/shard_map/while/body/eval_jaxpr/ppermute | solution.py:16
Sparse Core Ops, SparseCore 0:
  9.5 45.0 all-gather.2
  56.2 46.3 all-gather.4
where the time goes:
time: 366 us; the launch traced here: 364 us
  waiting for transfers between devices  185 us (51%)
  local copies, waits for them, and re-layouts  49.8 us (14%)
  starting transfers between devices  36.5 us (10%)
  other arithmetic  35.7 us (10%)
  matrix products  28.7 us (8%)
  loops' own time  14.3 us (4%)
  between operations  14.1 us (4%)
    ppermute x21, waiting for transfers between devices, from_behind(): return lax.ppermute(block, axis, route)  92.9 us
    all_gather x1, waiting for transfers between devices, per_device(): lax.all_gather(w_out, 'seq', axis=1, tiled=True)  47.9 us
    all_gather x1, waiting for transfers between devices, per_device(): lax.all_gather(w_query, 'seq', axis=2, tiled=True)  43.2 us
    ppermute x21, starting transfers between devices, from_behind(): return lax.ppermute(block, axis, route)  36.5 us
    dot_general x4, matrix products, project(): jnp.dot(normed, query_weight, preferred_element_type=jnp.float32)  15.5 us
    another operation x1, loops' own time, per_device(): final = lax.fori_loop(0, micro + sections - 1, turn, initial)  13.4 us
    dynamic_update_slice x7, other arithmetic, turn(): lax.dynamic_update_index_in_dim(cache_buffer, jnp.where(active, cache, pr...  7.9 us
    another operation x13, local copies, waits for them, and re-layouts  7.83 us
  transfers between devices with their start and end apart: 23, of which 9 were waited for; matrix products, arithmetic and copies ran while one was open for 8% of the time, Pallas kernels for 0%

commit v1 on v0

--- a/solution.py
+++ b/solution.py
@@ -37,8 +37,11 @@
     sections = lax.axis_size("section")
     seq_index = lax.axis_index("seq")
     micro, rows, width = tokens.shape
+    wrap_shifts_all = lambda slab_in, array_axis: jnp.concatenate(
+        jax.lax.all_gather(slab_in, "seq"), array_axis
+    )
     full_query, full_out = (
-        lax.all_gather(w_query, "seq", axis=2, tiled=True),
+        wrap_shifts_all(w_query, 2),
         lax.all_gather(w_out, "seq", axis=1, tiled=True),
     )
     query_weight = full_query[0]

time: 366 us -> 366 us (level)
  waiting for transfers between devices: 185 us -> 159 us
  local copies, waits for them, and re-layouts: 49.8 us -> 75.5 us
    all_gather x1, waiting for transfers between devices: 47.9 us -> 22.3 us  [per_device(): lax.all_gather(w_out, 'seq', axis=1, tiled=True)]
    reshape x0 -> x1, local copies, waits for them, and re-layouts: none -> 20.6 us  [per_device(): jnp.concatenate(jax.lax.all_gather(slab_in, 'seq'), array_axis)]
    unnamed x14 -> x15, local copies, waits for them, and re-layouts: 2.72 us -> 7.81 us
  transfers between devices with their start and end apart: 23 -> 23, of which waited for: 9 -> 9; matrix products, arithmetic and copies ran while one was open for 8% -> 15% of each run, Pallas kernels for 0% -> 0%
where the time goes in v1:
time: 366 us; the launch traced here: 364 us
  waiting for transfers between devices  159 us (43%)
  local copies, waits for them, and re-layouts  75.5 us (21%)
  starting transfers between devices  36.5 us (10%)
  other arithmetic  35.7 us (10%)
  matrix products  28.7 us (8%)
  loops' own time  14.5 us (4%)
  between operations  14.1 us (4%)
    ppermute x21, waiting for transfers between devices, from_behind(): return lax.ppermute(block, axis, route)  92.9 us
    all_gather x1, waiting for transfers between devices, per_device(): jax.lax.all_gather(slab_in, 'seq')  43.2 us
    ppermute x21, starting transfers between devices, from_behind(): return lax.ppermute(block, axis, route)  36.5 us
    all_gather x1, waiting for transfers between devices, per_device(): lax.all_gather(w_out, 'seq', axis=1, tiled=True)  22.3 us
    reshape x1, local copies, waits for them, and re-layouts, per_device(): jnp.concatenate(jax.lax.all_gather(slab_in, 'seq'), array_axis)  20.6 us
    dot_general x4, matrix products, project(): jnp.dot(normed, query_weight, preferred_element_type=jnp.float32)  15.5 us
    another operation x1, loops' own time, per_device(): final = lax.fori_loop(0, micro + sections - 1, turn, initial)  13.6 us
    dynamic_update_slice x7, other arithmetic, turn(): lax.dynamic_update_index_in_dim(cache_buffer, jnp.where(active, cache, pr...  7.9 us
  transfers between devices with their start and end apart: 23, of which 9 were waited for; matrix products, arithmetic and copies ran while one was open for 15% of the time, Pallas kernels for 0%

profile of v1, /device:TPU:28, one launch (start us, length us, event | category | flops | bytes accessed | tf_op | source)
XLA Modules:
  0.0 364.1 jit_solution(291645818742250799)
XLA Ops:
  8.5 1.6 copy.26
  11.5 43.2 %all-gather.6.cloned.1.call-done = bf16[4,1440,512]{2,1,0:T(8,128)(2,1)} async-done(((bf16[1,1440,512]{2,1,0:T(8,128)(2,1)}), bf16[4,1440,512]{2,1,0:T(8,128)(2,1)}) %all-gather.6.cloned.1.call-update) | async-done | bytes 5898256 | tf_op jit(solution)/shard_map/all_gather | solution.py:41
  54.6 20.6 %copy.25 = bf16[1,1440,4,512]{3,2,1,0:T(4,128)(2,1)S(1)} copy(bf16[1,1440,4,512]{3,1,2,0:T(8,128)(2,1)} %bitcast.84) | data formatting | bytes 11796480 | tf_op jit(solution)/shard_map/reshape | solution.py:40
  75.2 5.1 %copy.31 = bf16[180,8,4,512]{3,1,2,0:T(8,128)(2,1)} copy(bf16[180,8,4,512]{3,2,1,0:T(4,128)(2,1)S(1)} %bitcast.81) | data formatting | bytes 11796480
  80.3 22.3 %all-gather.4.cloned.1.call-done = bf16[1,2048,1440]{2,1,0:T(8,128)(2,1)} async-done(((bf16[1,512,1440]{2,1,0:T(8,128)(2,1)}), bf16[1,2048,1440]{2,1,0:T(8,128)(2,1)}) %all-gather.4.cloned.1.call-update) | async-done | bytes 5898256 | tf_op jit(solution)/shard_map/all_gather | solution.py:45
  104.3 252.9 %while.20 = (s32[]{:T(128)}, bf16[64,1440]{1,0:T(8,128)(2,1)S(1)}, bf16[4,64,1440]{2,1,0:T(8,128)(2,1)}, bf16[4,64,512]{2,1,0:T(8,128)(2,1)}, s32[]{:T(128)}, /*...) while((s32[]{:T(128)}, bf16[64,1440]{1,0:T(8,128)(2,1)S(1)}, ...), condition=%wide.region_8.9_spmd.clone.clone, body=%wide.region_0.8_spmd.clone.clone.sunk | while | flops 958372544 | bytes 47880768 | solution.py:146
  108.0 1.4 conditional.8
  109.3 2.5 collective-permute-start
  111.8 1.9 collective-permute-start.1
  116.2 1.3 collective-permute-start.2
  118.2 7.3 %collective-permute-done.2 = bf16[64,1440]{1,0:T(8,128)(2,1)S(1)} collective-permute-done((bf16[64,1440]{1,0:T(8,128)(2,1)S(1)}, bf16[64,1440]{1,0:T(8,128)(2,1)S(1)}, u32[]{:S(2)}, u32[]{:S(2)}) %collective-permute-start.2) | collective-permute-done | bytes 184352 | tf_op jit(solution)/shard_map/while/body/eval_jaxpr/ppermute | solution.py:16
  129.0 1.4 conditional.8
  130.3 3.0 collective-permute-start
  133.3 1.3 collective-permute-start.1
  137.1 1.3 collective-permute-start.2
  139.2 7.2 %collective-permute-done.2 = bf16[64,1440]{1,0:T(8,128)(2,1)S(1)} collective-permute-done((bf16[64,1440]{1,0:T(8,128)(2,1)S(1)}, bf16[64,1440]{1,0:T(8,128)(2,1)S(1)}, u32[]{:S(2)}, u32[]{:S(2)}) %collective-permute-start.2) | collective-permute-done | bytes 184352 | tf_op jit(solution)/shard_map/while/body/eval_jaxpr/ppermute | solution.py:16
  149.8 1.4 conditional.8
  151.2 3.0 collective-permute-start
  154.2 1.3 collective-permute-start.1
  158.0 1.3 collective-permute-start.2
  160.0 50.5 %collective-permute-done.2 = bf16[64,1440]{1,0:T(8,128)(2,1)S(1)} collective-permute-done((bf16[64,1440]{1,0:T(8,128)(2,1)S(1)}, bf16[64,1440]{1,0:T(8,128)(2,1)S(1)}, u32[]{:S(2)}, u32[]{:S(2)}) %collective-permute-start.2) | collective-permute-done | bytes 184352 | tf_op jit(solution)/shard_map/while/body/eval_jaxpr/ppermute | solution.py:16
  214.0 9.2 %conditional.8 = (bf16[64,2048]{1,0:T(8,128)(2,1)S(1)}, bf16[64,512]{1,0:T(8,128)(2,1)}, bf16[64,512]{0,1:T(8,128)(2,1)}) conditional(s32[]{:T(128)} %convert_element_type.69, () %tuple.81, (bf16[64,1440]{1,0:T(8,128)(2,1)S(1)}, f32[1,1440]{1,0:T(1,128)S(1)}, bf16[1440,2048]{1,0:T(8,128)(2,1)}, f32[64,1,32]{2,0,1:T(8,128)S(1)}, ...), branch_computations={%region_1.1_spmd, %region_2.3_spmd} | conditional | flops 474183744 | bytes 12373788 | solution.py:127
  214.2 3.9 %fusion.26 = f32[64,2048]{1,0:T(8,128)S(1)} fusion(bf16[1440,2048]{1,0:T(8,128)(2,1)} %get-tuple-element.374, bf16[64,1440]{1,0:T(8,128)(2,1)S(1)} %get-tuple-element.372, f32[1440]{0:T(1024)S(1)} %reduce, f32[64]{0:T(128)S(1)} %add_rsqrt_fusion), kind=kOutput, calls=%fused_computation.44 | convolution fusion | flops 377856000 | bytes 6612864 | tf_op jit(solution)/shard_map/while/body/eval_jaxpr/cond/branch_1_fun/dot_general | solution.py:68
  221.6 1.6 copy.30
  223.2 2.3 collective-permute-start
  225.5 1.3 collective-permute-start.1
  228.6 1.5 bitcast_dynamic-update-slice_fusion.5
  230.1 8.0 %conditional.9 = (bf16[64,1440]{1,0:T(8,128)(2,1)S(1)}) conditional(s32[]{:T(128)} %convert_element_type.69, bf16[64,1440]{1,0:T(8,128)(2,1)S(1)} %bitcast_select_fusion.5, (bf16[64,1440]{1,0:T(8,128)(2,1)S(1)}, bf16[64,512]{0,1:T(8,128)(2,1)S(1)}, bf16[64,512]{0,1:T(8,128)(2,1)S(1)}, bf16[64,512]{1,0:T(8,128)(2,1)}, s32[]{:T(128)}, ...), branch_computations={%region_4.4_spmd, %region_5.7_spmd} | conditional | flops 483969664 | bytes 32420688 | solution.py:129
  234.7 1.1 convolution_convert_fusion
  236.9 1.2 fusion.8
  238.2 1.3 collective-permute-start.2
  240.2 7.1 %collective-permute-done.2 = bf16[64,1440]{1,0:T(8,128)(2,1)S(1)} collective-permute-done((bf16[64,1440]{1,0:T(8,128)(2,1)S(1)}, bf16[64,1440]{1,0:T(8,128)(2,1)S(1)}, u32[]{:S(2)}, u32[]{:S(2)}) %collective-permute-start.2) | collective-permute-done | bytes 184352 | tf_op jit(solution)/shard_map/while/body/eval_jaxpr/ppermute | solution.py:16
  250.7 9.2 %conditional.8 = (bf16[64,2048]{1,0:T(8,128)(2,1)S(1)}, bf16[64,512]{1,0:T(8,128)(2,1)}, bf16[64,512]{0,1:T(8,128)(2,1)}) conditional(s32[]{:T(128)} %convert_element_type.69, () %tuple.81, (bf16[64,1440]{1,0:T(8,128)(2,1)S(1)}, f32[1,1440]{1,0:T(1,128)S(1)}, bf16[1440,2048]{1,0:T(8,128)(2,1)}, f32[64,1,32]{2,0,1:T(8,128)S(1)}, ...), branch_computations={%region_1.1_spmd, %region_2.3_spmd} | conditional | flops 474183744 | bytes 12373788 | solution.py:127
  250.9 3.9 %fusion.26 = f32[64,2048]{1,0:T(8,128)S(1)} fusion(bf16[1440,2048]{1,0:T(8,128)(2,1)} %get-tuple-element.374, bf16[64,1440]{1,0:T(8,128)(2,1)S(1)} %get-tuple-element.372, f32[1440]{0:T(1024)S(1)} %reduce, f32[64]{0:T(128)S(1)} %add_rsqrt_fusion), kind=kOutput, calls=%fused_computation.44 | convolution fusion | flops 377856000 | bytes 6612864 | tf_op jit(solution)/shard_map/while/body/eval_jaxpr/cond/branch_1_fun/dot_general | solution.py:68
  258.4 1.6 copy.30
  260.0 2.3 collective-permute-start
  262.3 1.3 collective-permute-start.1
  265.4 1.5 bitcast_dynamic-update-slice_fusion.5
  266.9 8.0 %conditional.9 = (bf16[64,1440]{1,0:T(8,128)(2,1)S(1)}) conditional(s32[]{:T(128)} %convert_element_type.69, bf16[64,1440]{1,0:T(8,128)(2,1)S(1)} %bitcast_select_fusion.5, (bf16[64,1440]{1,0:T(8,128)(2,1)S(1)}, bf16[64,512]{0,1:T(8,128)(2,1)S(1)}, bf16[64,512]{0,1:T(8,128)(2,1)S(1)}, bf16[64,512]{1,0:T(8,128)(2,1)}, s32[]{:T(128)}, ...), branch_computations={%region_4.4_spmd, %region_5.7_spmd} | conditional | flops 483969664 | bytes 32420688 | solution.py:129
  271.5 1.1 convolution_convert_fusion
  273.7 1.2 fusion.8
  274.9 1.3 collective-permute-start.2
  276.9 7.1 %collective-permute-done.2 = bf16[64,1440]{1,0:T(8,128)(2,1)S(1)} collective-permute-done((bf16[64,1440]{1,0:T(8,128)(2,1)S(1)}, bf16[64,1440]{1,0:T(8,128)(2,1)S(1)}, u32[]{:S(2)}, u32[]{:S(2)}) %collective-permute-start.2) | collective-permute-done | bytes 184352 | tf_op jit(solution)/shard_map/while/body/eval_jaxpr/ppermute | solution.py:16
  287.5 9.2 %conditional.8 = (bf16[64,2048]{1,0:T(8,128)(2,1)S(1)}, bf16[64,512]{1,0:T(8,128)(2,1)}, bf16[64,512]{0,1:T(8,128)(2,1)}) conditional(s32[]{:T(128)} %convert_element_type.69, () %tuple.81, (bf16[64,1440]{1,0:T(8,128)(2,1)S(1)}, f32[1,1440]{1,0:T(1,128)S(1)}, bf16[1440,2048]{1,0:T(8,128)(2,1)}, f32[64,1,32]{2,0,1:T(8,128)S(1)}, ...), branch_computations={%region_1.1_spmd, %region_2.3_spmd} | conditional | flops 474183744 | bytes 12373788 | solution.py:127
  287.7 3.9 %fusion.26 = f32[64,2048]{1,0:T(8,128)S(1)} fusion(bf16[1440,2048]{1,0:T(8,128)(2,1)} %get-tuple-element.374, bf16[64,1440]{1,0:T(8,128)(2,1)S(1)} %get-tuple-element.372, f32[1440]{0:T(1024)S(1)} %reduce, f32[64]{0:T(128)S(1)} %add_rsqrt_fusion), kind=kOutput, calls=%fused_computation.44 | convolution fusion | flops 377856000 | bytes 6612864 | tf_op jit(solution)/shard_map/while/body/eval_jaxpr/cond/branch_1_fun/dot_general | solution.py:68
  295.1 1.6 copy.30
  296.7 2.3 collective-permute-start
  299.0 1.3 collective-permute-start.1
  302.1 1.5 bitcast_dynamic-update-slice_fusion.5
  303.6 8.0 %conditional.9 = (bf16[64,1440]{1,0:T(8,128)(2,1)S(1)}) conditional(s32[]{:T(128)} %convert_element_type.69, bf16[64,1440]{1,0:T(8,128)(2,1)S(1)} %bitcast_select_fusion.5, (bf16[64,1440]{1,0:T(8,128)(2,1)S(1)}, bf16[64,512]{0,1:T(8,128)(2,1)S(1)}, bf16[64,512]{0,1:T(8,128)(2,1)S(1)}, bf16[64,512]{1,0:T(8,128)(2,1)}, s32[]{:T(128)}, ...), branch_computations={%region_4.4_spmd, %region_5.7_spmd} | conditional | flops 483969664 | bytes 32420688 | solution.py:129
  310.4 1.2 fusion.8
  311.7 1.3 collective-permute-start.2
  313.7 7.1 %collective-permute-done.2 = bf16[64,1440]{1,0:T(8,128)(2,1)S(1)} collective-permute-done((bf16[64,1440]{1,0:T(8,128)(2,1)S(1)}, bf16[64,1440]{1,0:T(8,128)(2,1)S(1)}, u32[]{:S(2)}, u32[]{:S(2)}) %collective-permute-start.2) | collective-permute-done | bytes 184352 | tf_op jit(solution)/shard_map/while/body/eval_jaxpr/ppermute | solution.py:16
  324.2 9.2 %conditional.8 = (bf16[64,2048]{1,0:T(8,128)(2,1)S(1)}, bf16[64,512]{1,0:T(8,128)(2,1)}, bf16[64,512]{0,1:T(8,128)(2,1)}) conditional(s32[]{:T(128)} %convert_element_type.69, () %tuple.81, (bf16[64,1440]{1,0:T(8,128)(2,1)S(1)}, f32[1,1440]{1,0:T(1,128)S(1)}, bf16[1440,2048]{1,0:T(8,128)(2,1)}, f32[64,1,32]{2,0,1:T(8,128)S(1)}, ...), branch_computations={%region_1.1_spmd, %region_2.3_spmd} | conditional | flops 474183744 | bytes 12373788 | solution.py:127
  324.4 3.9 %fusion.26 = f32[64,2048]{1,0:T(8,128)S(1)} fusion(bf16[1440,2048]{1,0:T(8,128)(2,1)} %get-tuple-element.374, bf16[64,1440]{1,0:T(8,128)(2,1)S(1)} %get-tuple-element.372, f32[1440]{0:T(1024)S(1)} %reduce, f32[64]{0:T(128)S(1)} %add_rsqrt_fusion), kind=kOutput, calls=%fused_computation.44 | convolution fusion | flops 377856000 | bytes 6612864 | tf_op jit(solution)/shard_map/while/body/eval_jaxpr/cond/branch_1_fun/dot_general | solution.py:68
  331.9 1.6 copy.30
  333.5 2.3 collective-permute-start
  335.8 1.3 collective-permute-start.1
  338.9 1.5 bitcast_dynamic-update-slice_fusion.5
  340.4 8.0 %conditional.9 = (bf16[64,1440]{1,0:T(8,128)(2,1)S(1)}) conditional(s32[]{:T(128)} %convert_element_type.69, bf16[64,1440]{1,0:T(8,128)(2,1)S(1)} %bitcast_select_fusion.5, (bf16[64,1440]{1,0:T(8,128)(2,1)S(1)}, bf16[64,512]{0,1:T(8,128)(2,1)S(1)}, bf16[64,512]{0,1:T(8,128)(2,1)S(1)}, bf16[64,512]{1,0:T(8,128)(2,1)}, s32[]{:T(128)}, ...), branch_computations={%region_4.4_spmd, %region_5.7_spmd} | conditional | flops 483969664 | bytes 32420688 | solution.py:129
  345.0 1.1 convolution_convert_fusion
  347.2 1.2 fusion.8
  348.4 1.3 collective-permute-start.2
  350.4 6.8 %collective-permute-done.2 = bf16[64,1440]{1,0:T(8,128)(2,1)S(1)} collective-permute-done((bf16[64,1440]{1,0:T(8,128)(2,1)S(1)}, bf16[64,1440]{1,0:T(8,128)(2,1)S(1)}, u32[]{:S(2)}, u32[]{:S(2)}) %collective-permute-start.2) | collective-permute-done | bytes 184352 | tf_op jit(solution)/shard_map/while/body/eval_jaxpr/ppermute | solution.py:16
  (246 shorter events, 77.4 us)
Async XLA Ops:
  7.2 1.4 copy-start.1
  7.2 47.5 %all-gather.6.cloned.1.call-start = ((), (), s32[]{:S(2)}) async-start(), calls=%async_computation.1 | async-start | bytes 7372800 | tf_op jit(solution)/shard_map/all_gather | solution.py:41
  7.9 2.8 copy-start.3
  7.9 94.7 %all-gather.4.cloned.1.call-start = ((), (), s32[]{:S(2)}) async-start(), calls=%async_computation | async-start | bytes 7864320 | tf_op jit(solution)/shard_map/all_gather | solution.py:45
  75.2 29.1 %copy-start = (bf16[1,1440,512]{2,1,0:T(8,128)(2,1)S(1)}, bf16[1,1440,512]{2,1,0:T(8,128)(2,1)}, u32[]{:S(2)}) copy-start(bf16[1,1440,512]{2,1,0:T(8,128)(2,1)} %param.19) | copy-start | bytes 4423684
  75.2 29.1 %copy-start.2 = (f32[1,1440]{1,0:T(1,128)S(1)}, f32[1,1440]{1,0:T(1,128)}, u32[]{:S(2)}) copy-start(f32[1,1440]{1,0:T(1,128)} %param.17) | copy-start | bytes 17284
  75.2 29.1 %copy-start.4 = (s32[4]{0:T(128)S(1)}, s32[4]{0:T(128)}, u32[]{:S(2)}) copy-start(s32[4]{0:T(128)} %param.15) | copy-start | bytes 52
  75.2 29.0 %copy-start.5 = (s32[4]{0:T(128)S(1)}, s32[4]{0:T(128)}, u32[]{:S(2)}) copy-start(s32[4]{0:T(128)} %param.16) | copy-start | bytes 52
  109.3 6.8 %collective-permute-start = (bf16[64,512]{0,1:T(8,128)(2,1)}, bf16[64,512]{0,1:T(8,128)(2,1)S(1)}, u32[]{:S(2)}, u32[]{:S(2)}) collective-permute-start(bf16[64,512]{0,1:T(8,128)(2,1)} %get-tuple-element.718), channel_id=1, source_target_pairs={{0,2},{1,3},{4,6},{5,7},{8,10},{9,11},{12,14},{13,15},{16,18},{17,... | collective-permute-start | bytes 196616 | tf_op jit(solution)/shard_map/while/body/eval_jaxpr/ppermute | solution.py:16
  111.8 4.3 %collective-permute-start.1 = (bf16[64,512]{0,1:T(8,128)(2,1)}, bf16[64,512]{0,1:T(8,128)(2,1)S(1)}, u32[]{:S(2)}, u32[]{:S(2)}) collective-permute-start(bf16[64,512]{0,1:T(8,128)(2,1)} %get-tuple-element.718), channel_id=1, source_target_pairs={{0,1},{1,2},{2,3},{4,5},{5,6},{6,7},{8,9},{9,10},{10,11},{12,13},{... | collective-permute-start | bytes 196616 | tf_op jit(solution)/shard_map/while/body/eval_jaxpr/ppermute | solution.py:16
  116.2 9.3 %collective-permute-start.2 = (bf16[64,1440]{1,0:T(8,128)(2,1)S(1)}, bf16[64,1440]{1,0:T(8,128)(2,1)S(1)}, u32[]{:S(2)}, u32[]{:S(2)}) collective-permute-start(bf16[64,1440]{1,0:T(8,128)(2,1)S(1)} %get-tuple-element.793), channel_id=1, source_target_pairs={{0,4},{4,8},{8,12},{1,5},{5,9},{9,13},{2,6},{6,10},{10,14},{3,7},{... | collective-permute-start | bytes 552968 | tf_op jit(solution)/shard_map/while/body/eval_jaxpr/ppermute | solution.py:16
  130.3 6.8 %collective-permute-start = (bf16[64,512]{0,1:T(8,128)(2,1)}, bf16[64,512]{0,1:T(8,128)(2,1)S(1)}, u32[]{:S(2)}, u32[]{:S(2)}) collective-permute-start(bf16[64,512]{0,1:T(8,128)(2,1)} %get-tuple-element.718), channel_id=1, source_target_pairs={{0,2},{1,3},{4,6},{5,7},{8,10},{9,11},{12,14},{13,15},{16,18},{17,... | collective-permute-start | bytes 196616 | tf_op jit(solution)/shard_map/while/body/eval_jaxpr/ppermute | solution.py:16
  133.3 3.8 %collective-permute-start.1 = (bf16[64,512]{0,1:T(8,128)(2,1)}, bf16[64,512]{0,1:T(8,128)(2,1)S(1)}, u32[]{:S(2)}, u32[]{:S(2)}) collective-permute-start(bf16[64,512]{0,1:T(8,128)(2,1)} %get-tuple-element.718), channel_id=1, source_target_pairs={{0,1},{1,2},{2,3},{4,5},{5,6},{6,7},{8,9},{9,10},{10,11},{12,13},{... | collective-permute-start | bytes 196616 | tf_op jit(solution)/shard_map/while/body/eval_jaxpr/ppermute | solution.py:16
  137.1 9.2 %collective-permute-start.2 = (bf16[64,1440]{1,0:T(8,128)(2,1)S(1)}, bf16[64,1440]{1,0:T(8,128)(2,1)S(1)}, u32[]{:S(2)}, u32[]{:S(2)}) collective-permute-start(bf16[64,1440]{1,0:T(8,128)(2,1)S(1)} %get-tuple-element.793), channel_id=1, source_target_pairs={{0,4},{4,8},{8,12},{1,5},{5,9},{9,13},{2,6},{6,10},{10,14},{3,7},{... | collective-permute-start | bytes 552968 | tf_op jit(solution)/shard_map/while/body/eval_jaxpr/ppermute | solution.py:16
  151.2 6.8 %collective-permute-start = (bf16[64,512]{0,1:T(8,128)(2,1)}, bf16[64,512]{0,1:T(8,128)(2,1)S(1)}, u32[]{:S(2)}, u32[]{:S(2)}) collective-permute-start(bf16[64,512]{0,1:T(8,128)(2,1)} %get-tuple-element.718), channel_id=1, source_target_pairs={{0,2},{1,3},{4,6},{5,7},{8,10},{9,11},{12,14},{13,15},{16,18},{17,... | collective-permute-start | bytes 196616 | tf_op jit(solution)/shard_map/while/body/eval_jaxpr/ppermute | solution.py:16
  154.2 3.8 %collective-permute-start.1 = (bf16[64,512]{0,1:T(8,128)(2,1)}, bf16[64,512]{0,1:T(8,128)(2,1)S(1)}, u32[]{:S(2)}, u32[]{:S(2)}) collective-permute-start(bf16[64,512]{0,1:T(8,128)(2,1)} %get-tuple-element.718), channel_id=1, source_target_pairs={{0,1},{1,2},{2,3},{4,5},{5,6},{6,7},{8,9},{9,10},{10,11},{12,13},{... | collective-permute-start | bytes 196616 | tf_op jit(solution)/shard_map/while/body/eval_jaxpr/ppermute | solution.py:16
  158.0 52.5 %collective-permute-start.2 = (bf16[64,1440]{1,0:T(8,128)(2,1)S(1)}, bf16[64,1440]{1,0:T(8,128)(2,1)S(1)}, u32[]{:S(2)}, u32[]{:S(2)}) collective-permute-start(bf16[64,1440]{1,0:T(8,128)(2,1)S(1)} %get-tuple-element.793), channel_id=1, source_target_pairs={{0,4},{4,8},{8,12},{1,5},{5,9},{9,13},{2,6},{6,10},{10,14},{3,7},{... | collective-permute-start | bytes 552968 | tf_op jit(solution)/shard_map/while/body/eval_jaxpr/ppermute | solution.py:16
  223.2 6.9 %collective-permute-start = (bf16[64,512]{0,1:T(8,128)(2,1)}, bf16[64,512]{0,1:T(8,128)(2,1)S(1)}, u32[]{:S(2)}, u32[]{:S(2)}) collective-permute-start(bf16[64,512]{0,1:T(8,128)(2,1)} %get-tuple-element.718), channel_id=1, source_target_pairs={{0,2},{1,3},{4,6},{5,7},{8,10},{9,11},{12,14},{13,15},{16,18},{17,... | collective-permute-start | bytes 196616 | tf_op jit(solution)/shard_map/while/body/eval_jaxpr/ppermute | solution.py:16
  225.5 4.6 %collective-permute-start.1 = (bf16[64,512]{0,1:T(8,128)(2,1)}, bf16[64,512]{0,1:T(8,128)(2,1)S(1)}, u32[]{:S(2)}, u32[]{:S(2)}) collective-permute-start(bf16[64,512]{0,1:T(8,128)(2,1)} %get-tuple-element.718), channel_id=1, source_target_pairs={{0,1},{1,2},{2,3},{4,5},{5,6},{6,7},{8,9},{9,10},{10,11},{12,13},{... | collective-permute-start | bytes 196616 | tf_op jit(solution)/shard_map/while/body/eval_jaxpr/ppermute | solution.py:16
  233.8 2.2 slice-start
  234.7 2.2 slice-start.1
  238.2 9.1 %collective-permute-start.2 = (bf16[64,1440]{1,0:T(8,128)(2,1)S(1)}, bf16[64,1440]{1,0:T(8,128)(2,1)S(1)}, u32[]{:S(2)}, u32[]{:S(2)}) collective-permute-start(bf16[64,1440]{1,0:T(8,128)(2,1)S(1)} %get-tuple-element.793), channel_id=1, source_target_pairs={{0,4},{4,8},{8,12},{1,5},{5,9},{9,13},{2,6},{6,10},{10,14},{3,7},{... | collective-permute-start | bytes 552968 | tf_op jit(solution)/shard_map/while/body/eval_jaxpr/ppermute | solution.py:16
  260.0 6.9 %collective-permute-start = (bf16[64,512]{0,1:T(8,128)(2,1)}, bf16[64,512]{0,1:T(8,128)(2,1)S(1)}, u32[]{:S(2)}, u32[]{:S(2)}) collective-permute-start(bf16[64,512]{0,1:T(8,128)(2,1)} %get-tuple-element.718), channel_id=1, source_target_pairs={{0,2},{1,3},{4,6},{5,7},{8,10},{9,11},{12,14},{13,15},{16,18},{17,... | collective-permute-start | bytes 196616 | tf_op jit(solution)/shard_map/while/body/eval_jaxpr/ppermute | solution.py:16
  262.3 4.6 %collective-permute-start.1 = (bf16[64,512]{0,1:T(8,128)(2,1)}, bf16[64,512]{0,1:T(8,128)(2,1)S(1)}, u32[]{:S(2)}, u32[]{:S(2)}) collective-permute-start(bf16[64,512]{0,1:T(8,128)(2,1)} %get-tuple-element.718), channel_id=1, source_target_pairs={{0,1},{1,2},{2,3},{4,5},{5,6},{6,7},{8,9},{9,10},{10,11},{12,13},{... | collective-permute-start | bytes 196616 | tf_op jit(solution)/shard_map/while/body/eval_jaxpr/ppermute | solution.py:16
  270.6 2.2 slice-start
  271.5 2.2 slice-start.1
  274.9 9.1 %collective-permute-start.2 = (bf16[64,1440]{1,0:T(8,128)(2,1)S(1)}, bf16[64,1440]{1,0:T(8,128)(2,1)S(1)}, u32[]{:S(2)}, u32[]{:S(2)}) collective-permute-start(bf16[64,1440]{1,0:T(8,128)(2,1)S(1)} %get-tuple-element.793), channel_id=1, source_target_pairs={{0,4},{4,8},{8,12},{1,5},{5,9},{9,13},{2,6},{6,10},{10,14},{3,7},{... | collective-permute-start | bytes 552968 | tf_op jit(solution)/shard_map/while/body/eval_jaxpr/ppermute | solution.py:16
  296.7 6.9 %collective-permute-start = (bf16[64,512]{0,1:T(8,128)(2,1)}, bf16[64,512]{0,1:T(8,128)(2,1)S(1)}, u32[]{:S(2)}, u32[]{:S(2)}) collective-permute-start(bf16[64,512]{0,1:T(8,128)(2,1)} %get-tuple-element.718), channel_id=1, source_target_pairs={{0,2},{1,3},{4,6},{5,7},{8,10},{9,11},{12,14},{13,15},{16,18},{17,... | collective-permute-start | bytes 196616 | tf_op jit(solution)/shard_map/while/body/eval_jaxpr/ppermute | solution.py:16
  299.0 4.6 %collective-permute-start.1 = (bf16[64,512]{0,1:T(8,128)(2,1)}, bf16[64,512]{0,1:T(8,128)(2,1)S(1)}, u32[]{:S(2)}, u32[]{:S(2)}) collective-permute-start(bf16[64,512]{0,1:T(8,128)(2,1)} %get-tuple-element.718), channel_id=1, source_target_pairs={{0,1},{1,2},{2,3},{4,5},{5,6},{6,7},{8,9},{9,10},{10,11},{12,13},{... | collective-permute-start | bytes 196616 | tf_op jit(solution)/shard_map/while/body/eval_jaxpr/ppermute | solution.py:16
  307.3 2.2 slice-start
  308.2 2.2 slice-start.1
  311.7 9.1 %collective-permute-start.2 = (bf16[64,1440]{1,0:T(8,128)(2,1)S(1)}, bf16[64,1440]{1,0:T(8,128)(2,1)S(1)}, u32[]{:S(2)}, u32[]{:S(2)}) collective-permute-start(bf16[64,1440]{1,0:T(8,128)(2,1)S(1)} %get-tuple-element.793), channel_id=1, source_target_pairs={{0,4},{4,8},{8,12},{1,5},{5,9},{9,13},{2,6},{6,10},{10,14},{3,7},{... | collective-permute-start | bytes 552968 | tf_op jit(solution)/shard_map/while/body/eval_jaxpr/ppermute | solution.py:16
  333.5 6.9 %collective-permute-start = (bf16[64,512]{0,1:T(8,128)(2,1)}, bf16[64,512]{0,1:T(8,128)(2,1)S(1)}, u32[]{:S(2)}, u32[]{:S(2)}) collective-permute-start(bf16[64,512]{0,1:T(8,128)(2,1)} %get-tuple-element.718), channel_id=1, source_target_pairs={{0,2},{1,3},{4,6},{5,7},{8,10},{9,11},{12,14},{13,15},{16,18},{17,... | collective-permute-start | bytes 196616 | tf_op jit(solution)/shard_map/while/body/eval_jaxpr/ppermute | solution.py:16
  335.8 4.6 %collective-permute-start.1 = (bf16[64,512]{0,1:T(8,128)(2,1)}, bf16[64,512]{0,1:T(8,128)(2,1)S(1)}, u32[]{:S(2)}, u32[]{:S(2)}) collective-permute-start(bf16[64,512]{0,1:T(8,128)(2,1)} %get-tuple-element.718), channel_id=1, source_target_pairs={{0,1},{1,2},{2,3},{4,5},{5,6},{6,7},{8,9},{9,10},{10,11},{12,13},{... | collective-permute-start | bytes 196616 | tf_op jit(solution)/shard_map/while/body/eval_jaxpr/ppermute | solution.py:16
  344.1 2.2 slice-start
  345.0 2.2 slice-start.1
  348.4 8.8 %collective-permute-start.2 = (bf16[64,1440]{1,0:T(8,128)(2,1)S(1)}, bf16[64,1440]{1,0:T(8,128)(2,1)S(1)}, u32[]{:S(2)}, u32[]{:S(2)}) collective-permute-start(bf16[64,1440]{1,0:T(8,128)(2,1)S(1)} %get-tuple-element.793), channel_id=1, source_target_pairs={{0,4},{4,8},{8,12},{1,5},{5,9},{9,13},{2,6},{6,10},{10,14},{3,7},{... | collective-permute-start | bytes 552968 | tf_op jit(solution)/shard_map/while/body/eval_jaxpr/ppermute | solution.py:16
Sparse Core Ops, SparseCore 0:
  9.5 45.0 all-gather.5
  56.2 46.3 all-gather.3
